TPU v7x, 256 devices: a whole 4x4x8 slice. The times are simulated.
256 devices in a mesh: grid: 8 (over z), orb: 16 (over y, x_hi, core), pts: 2 (over x_lo).
Axes of the slice: x: 4 (x_hi: 2, x_lo: 2; x = x_hi * 2 + x_lo), y: 4, z: 8, core: 2. Of those that a mesh axis runs over, the one named last changes fastest.
Arguments:
- orbitals: bfloat16 [2048, 2048], P('grid', 'orb'), may hold values from -6 to 6
- points: int32 [8192], replicated, may hold values from 0 to 2047
- fitting: bfloat16 [2048, 8192], P('grid', ('orb', 'pts')), may hold values from -0.0625 to 0.0625
- screened: bfloat16 [8192, 8192], P(('orb', 'pts'), 'grid'), may hold values from -0.0014648438 to 0.0014648438
Outputs:
- exchange_orbitals: float32 [2048, 2048], P(('orb', 'pts'), 'grid')
- exchange_matrix: float32 [2048, 2048], P(('orb', 'pts'), 'grid')
Inputs may be any that keep to these rules, and one draw needn't show every extreme that they name: Grid rows of the window; two points may name the same row.
All inputs are finite; a program needn't handle non-finite values.
Results may differ from a plain program's by a relative error of at most 0.005.
Values may be sent and summed in bfloat16 or wider, within the bound.
No kernel may reach another device: no remote copies, remote signals or barrier semaphores. Data moves between devices by JAX's collectives and lax.ppermute only.
A program may use at most 128 MiB of HBM per device.

v0:
```python
import math

import jax
import jax.numpy as jnp
from jax import lax
from jax.sharding import PartitionSpec as P


def in_one_piece(arrays, axis, dim, along):
    widths = [a.shape[along] for a in arrays]
    both = jnp.concatenate(arrays, axis=along)
    filled = lax.all_gather(both, axis, axis=dim, tiled=True)
    return tuple(jnp.split(filled, [sum(widths[:k]) for k in range(1, len(widths))], axis=along))


def laid_out(parts, dim):
    parts = jnp.moveaxis(parts, 0, dim)
    shape = parts.shape
    return parts.reshape(*shape[:dim], shape[dim] * shape[dim + 1], *shape[dim + 2 :])


def sent_to_all(x, axis):
    copies = jnp.broadcast_to(x, (lax.axis_size(axis), *x.shape))
    return lax.all_to_all(copies, axis, split_axis=0, concat_axis=0, tiled=True)


def collect(x, axis, dim):
    return laid_out(sent_to_all(x, axis), dim)


def split_up(x, dim, peers):
    shape = x.shape
    parts = x.reshape(*shape[:dim], peers, shape[dim] // peers, *shape[dim + 1 :])
    return jnp.moveaxis(parts, dim, 0)


def sent_and_summed(x, axis, dim):
    peers = lax.axis_size(axis)
    parts = lax.all_to_all(split_up(x, dim, peers), axis, 0, 0, tiled=True)
    return jnp.sum(parts, axis=0)


def per_device(orbitals, points, fitting, screened):
    grid_index = lax.axis_index("grid")
    orb_index = lax.axis_index("orb")
    pts_index = lax.axis_index("pts")
    n_grid = lax.axis_size("grid")
    n_orb = lax.axis_size("orb")
    n_pts = lax.axis_size("pts")
    rows_dev, width_dev = orbitals.shape
    npoints = points.shape[0]
    nfull = width_dev * n_orb
    point_block = npoints // (n_orb * n_pts)
    column_block = npoints // n_grid
    orbital_block = nfull // (n_orb * n_pts)
    local_rows = points - grid_index * rows_dev
    inside = (local_rows >= 0) & (local_rows < rows_dev)
    clamped = jnp.clip(local_rows, 0, rows_dev - 1)
    taken = jnp.take(orbitals, clamped, axis=0).astype(jnp.float32)
    selected = jnp.where(inside[:, None], taken, jnp.zeros_like(taken))
    picked = lax.psum(selected.astype(jnp.bfloat16), "grid")
    grouped = picked.reshape(n_orb, n_pts, point_block, width_dev)
    own_rows = lax.dynamic_index_in_dim(grouped, pts_index, 1, keepdims=False).reshape(
        n_orb * point_block, width_dev
    )
    point_rows = lax.dynamic_slice_in_dim(picked, grid_index * column_block, column_block, 0)
    rows_full, point_full = in_one_piece((own_rows, point_rows), "orb", 1, 0)
    own_full = lax.dynamic_slice_in_dim(rows_full, orb_index * point_block, point_block, 0)
    density = lax.dot_general(
        own_full, point_full, (((1,), (1,)), ((), ())), preferred_element_type=jnp.float32
    )
    masked = (density * screened.astype(jnp.float32)).astype(jnp.bfloat16)
    partial_applied = jnp.dot(masked, point_full, preferred_element_type=jnp.float32)
    applied = lax.psum(partial_applied, "grid").astype(jnp.bfloat16)
    columns = lax.all_to_all(applied, ("orb", "pts"), split_axis=1, concat_axis=0, tiled=True)
    initial = jnp.zeros((orbital_block, rows_dev), jnp.float32)
    terms = initial - lax.dot_general(
        columns,
        lax.all_gather(fitting, ("orb", "pts"), axis=1, tiled=True),
        (((0,), (1,)), ((), ())),
        preferred_element_type=jnp.float32,
    )
    rounded = terms.astype(jnp.bfloat16)
    partial_matrix = jnp.dot(
        rounded, collect(orbitals, "orb", 1), preferred_element_type=jnp.float32
    )
    summed = sent_and_summed(partial_matrix, "grid", 1)
    exchange_matrix = summed / math.sqrt(rows_dev * n_grid)
    return (terms, exchange_matrix)


def solution(mesh):
    in_specs = (P("grid", "orb"), P(), P("grid", ("orb", "pts")), P(("orb", "pts"), "grid"))
    out_specs = (P(("orb", "pts"), "grid"), P(("orb", "pts"), "grid"))
    return jax.shard_map(
        per_device, mesh=mesh, in_specs=in_specs, out_specs=out_specs, check_vma=False
    )
```

profile of v0, /device:TPU:1, one launch (start us, length us, event | category | flops | bytes accessed | tf_op | source)
XLA Modules:
  0.0 432.1 jit_solution(11468976855244154880)
XLA Ops:
  7.2 0.0 copy-start
  7.2 0.0 all-reduce.3.cloned.1.call-start
  7.2 0.8 compare_and_fusion.1
  8.0 0.8 fusion.17
  8.8 0.0 copy-done
  8.8 24.0 %gather_fusion = bf16[8192,128]{1,0:T(8,128)(2,1)S(1)} fusion(bf16[256,128]{1,0:T(8,128)(2,1)S(1)} %copy-done, s32[8192]{0:T(1024)S(1)} %fusion.17), kind=kCustom, calls=%fused_computation | custom fusion | bytes 4227072 | tf_op jit(solution)/shard_map/jit(_take)/gather | solution.py:59
  32.9 6.7 %select_convert_fusion = bf16[8192,128]{1,0:T(8,128)(2,1)} fusion(bf16[8192,128]{1,0:T(8,128)(2,1)S(1)} %gather_fusion, pred[8192]{0:T(1024)(128)(4,1)S(1)} %get-tuple-element.3, pred[8192]{0:T(1024)(128)(4,1)S(1)} %get-tuple-element.2), kind=kLoop, calls=%fused_computation.1 | loop fusion | flops 4194304 | bytes 4210688 | tf_op jit(solution)/shard_map/convert_element_type | solution.py:61
  39.6 0.0 all-reduce.3.cloned.1.call-update
  39.6 0.0 all-gather.3.cloned.1.call-start
  39.7 82.1 %all-reduce.3.cloned.1.call-done = bf16[8192,128]{1,0:T(8,128)(2,1)} async-done(((bf16[8192,128]{1,0:T(8,128)(2,1)}), bf16[8192,128]{1,0:T(8,128)(2,1)}) %all-reduce.3.cloned.1.call-update) | async-done | bytes 2097168 | tf_op jit(solution)/shard_map/psum | solution.py:61
  121.8 1.3 constant_dynamic-slice_fusion.1
  123.1 1.0 constant_dynamic-slice_fusion
  124.1 1.2 pad_maximum_fusion
  125.2 0.0 all-gather.3.cloned.1.call-update
  125.3 0.0 all-gather.5.cloned.1.call-start
  125.3 0.7 all-gather.5.cloned.1.call-update
  126.0 0.0 copy-start.2
  126.0 147.0 %all-gather.3.cloned.1.call-done = bf16[5120,2048]{1,0:T(8,128)(2,1)} async-done(((bf16[5120,128]{1,0:T(8,128)(2,1)}), bf16[5120,2048]{1,0:T(8,128)(2,1)}) %all-gather.3.cloned.1.call-update) | async-done | bytes 20971536 | tf_op jit(solution)/shard_map/all_gather | solution.py:12
  273.0 14.2 %split.8 = bf16[4096,2048]{1,0:T(8,128)(2,1)} slice(bf16[5120,2048]{1,0:T(8,128)(2,1)} %all-gather.3.cloned.1.call-done), slice={[0:4096], [0:2048]} | slice | bytes 33554432 | tf_op jit(solution)/shard_map/split | solution.py:13
  287.2 0.0 copy-done.2
  287.3 6.2 %fusion = f32[256,2048]{1,0:T(8,128)S(1)} fusion(bf16[5120,2048]{1,0:T(8,128)(2,1)} %all-gather.3.cloned.1.call-done, bf16[256,1024]{1,0:T(8,128)(2,1)S(1)} %copy-done.2, bf16[4096,2048]{1,0:T(8,128)(2,1)} %split.8, s32[]{:T(128)S(6)} %select_n.28), kind=kOutput, calls=%fused_computation.2 | convolution fusion | flops 2148270080 | bytes 12058628 | tf_op jit(solution)/shard_map/dot_general | solution.py:73
  293.5 55.7 %all-reduce.4 = bf16[256,2048]{1,0:T(8,128)(2,1)S(1)} all-reduce(f32[256,2048]{1,0:T(8,128)S(1)} %fusion), channel_id=1, replica_groups=mesh['grid'=8,'orb'=16,'pts'=2] {'grid'}, use_global_device_ids=true, to_apply=%region_1.2 | all-reduce | flops 524288 | bytes 3145728 | tf_op jit(solution)/shard_map/psum | solution.py:74
  349.2 1.3 copy.7
  350.5 15.2 %all-to-all-start = ((bf16[256,32,64]{0,2,1:T(8,128)(2,1)}), bf16[256,32,64]{0,2,1:T(8,128)(2,1)S(1)}, u32[]{:S(2)}, u32[]{:S(2)}) async-start(bf16[256,32,64]{0,2,1:T(8,128)(2,1)} %bitcast.2), calls=%async_computation | async-start | bytes 2097152 | tf_op jit(solution)/shard_map/all_to_all | solution.py:75
  365.7 0.1 copy.9
  365.8 15.6 %all-to-all-done = bf16[256,32,64]{0,2,1:T(8,128)(2,1)S(1)} async-done(((bf16[256,32,64]{0,2,1:T(8,128)(2,1)}), bf16[256,32,64]{0,2,1:T(8,128)(2,1)S(1)}, u32[]{:S(2)}, u32[]{:S(2)}) %all-to-all-start) | async-done | bytes 1048608 | tf_op jit(solution)/shard_map/all_to_all | solution.py:75
  381.4 1.1 broadcast_in_dim.36
  382.5 6.0 %all-to-all-start.1 = ((bf16[16,256,128]{1,2,0:T(8,128)(2,1)}), bf16[16,256,128]{1,2,0:T(8,128)(2,1)S(1)}, u32[]{:S(2)}, u32[]{:S(2)}) async-start(bf16[16,256,128]{1,2,0:T(8,128)(2,1)} %broadcast_in_dim.36), calls=%async_computation.1 | async-start | bytes 2097152 | tf_op jit(solution)/shard_map/all_to_all | solution.py:24
  388.5 0.1 copy.10
  388.6 0.0 all-gather.5.cloned.1.call-done
  388.6 3.6 convolution_subtract_fusion
  392.2 0.0 copy-start.1
  392.2 13.4 %all-to-all-done.1 = bf16[16,256,128]{1,2,0:T(8,128)(2,1)S(1)} async-done(((bf16[16,256,128]{1,2,0:T(8,128)(2,1)}), bf16[16,256,128]{1,2,0:T(8,128)(2,1)S(1)}, u32[]{:S(2)}, u32[]{:S(2)}) %all-to-all-start.1) | async-done | bytes 1048608 | tf_op jit(solution)/shard_map/all_to_all | solution.py:24
  405.6 0.4 convolution_bitcast_fusion
  406.0 18.9 %all_to_all.29 = f32[8,64,256]{2,1,0:T(8,128)S(1)} all-to-all(f32[8,64,256]{2,1,0:T(8,128)S(1)} %convolution_bitcast_fusion), channel_id=1, replica_groups=mesh['grid'=8,'orb'=16,'pts'=2] {'grid'}, dimensions={0} | all-to-all | bytes 1048576 | tf_op jit(solution)/shard_map/all_to_all | solution.py:39
  424.9 0.6 broadcast_multiply_fusion
  425.6 0.0 copy-done.1
  (1 shorter events, 0.0 us)
Async XLA Ops:
  7.2 1.6 copy-start
  7.2 114.6 %all-reduce.3.cloned.1.call-start = ((), (), s32[]{:S(2)}) async-start(), calls=%async_computation.3 | async-start | bytes 4194304 | tf_op jit(solution)/shard_map/psum | solution.py:61
  39.6 233.4 %all-gather.3.cloned.1.call-start = ((), (), s32[]{:S(2)}) async-start(), calls=%async_computation.4 | async-start | bytes 22282240 | tf_op jit(solution)/shard_map/all_gather | solution.py:12
  125.3 263.3 %all-gather.5.cloned.1.call-start = ((), (), s32[]{:S(2)}) async-start(), calls=%async_computation.5 | async-start | bytes 4325376 | tf_op jit(solution)/shard_map/all_gather | solution.py:79
  126.0 161.3 %copy-start.2 = (bf16[256,1024]{1,0:T(8,128)(2,1)S(1)}, bf16[256,1024]{1,0:T(8,128)(2,1)}, u32[]{:S(2)}) copy-start(bf16[256,1024]{1,0:T(8,128)(2,1)} %param.7) | copy-start | bytes 1572868
  350.5 30.9 %all-to-all-start = ((bf16[256,32,64]{0,2,1:T(8,128)(2,1)}), bf16[256,32,64]{0,2,1:T(8,128)(2,1)S(1)}, u32[]{:S(2)}, u32[]{:S(2)}) async-start(bf16[256,32,64]{0,2,1:T(8,128)(2,1)} %bitcast.2), calls=%async_computation | async-start | bytes 2097152 | tf_op jit(solution)/shard_map/all_to_all | solution.py:75
  382.5 23.1 %all-to-all-start.1 = ((bf16[16,256,128]{1,2,0:T(8,128)(2,1)}), bf16[16,256,128]{1,2,0:T(8,128)(2,1)S(1)}, u32[]{:S(2)}, u32[]{:S(2)}) async-start(bf16[16,256,128]{1,2,0:T(8,128)(2,1)} %broadcast_in_dim.36), calls=%async_computation.1 | async-start | bytes 2097152 | tf_op jit(solution)/shard_map/all_to_all | solution.py:24
  392.2 33.4 %copy-start.1 = (f32[64,256]{1,0:T(8,128)}, f32[64,256]{1,0:T(8,128)S(1)}, u32[]{:S(2)}) copy-start(f32[64,256]{1,0:T(8,128)S(1)} %convolution_subtract_fusion) | copy-start | bytes 196612
Sparse Core Ops, SparseCore 0:
  39.7 82.0 all-reduce.2
  125.4 147.6 all-gather.2
  274.8 82.4 all-gather.4
where the time goes:
time: 433 us; the launch traced here: 432 us
  waiting for transfers between devices  259 us (60%)
  blocking collectives  74.6 us (17%)
  local copies, waits for them, and re-layouts  43.1 us (10%)
  starting transfers between devices  21.3 us (5%)
  between operations  13.9 us (3%)
  matrix products  10.2 us (2%)
  other arithmetic  10.1 us (2%)
    all_gather x1, waiting for transfers between devices, in_one_piece(): filled = lax.all_gather(both, axis, axis=dim, tiled=True)  147 us
    psum x1, waiting for transfers between devices, per_device(): picked = lax.psum(selected.astype(jnp.bfloat16), 'grid')  82.1 us
    psum x1, blocking collectives, per_device(): applied = lax.psum(partial_applied, 'grid').astype(jnp.bfloat16)  55.7 us
    gather x1, local copies, waits for them, and re-layouts, per_device(): taken = jnp.take(orbitals, clamped, axis=0).astype(jnp.float32)  24 us
    all_to_all x1, blocking collectives, sent_and_summed(): parts = lax.all_to_all(split_up(x, dim, peers), axis, 0, 0, tiled=True)  18.9 us
    all_to_all x1, waiting for transfers between devices, per_device(): lax.all_to_all(applied, ('orb', 'pts'), split_axis=1, concat_axis=0, tile...  15.6 us
    all_to_all x1, starting transfers between devices, per_device(): lax.all_to_all(applied, ('orb', 'pts'), split_axis=1, concat_axis=0, tile...  15.2 us
    split x1, local copies, waits for them, and re-layouts, in_one_piece(): jnp.split(filled, [sum(widths[:k]) for k in range(1, len(widths))], axis=...  14.2 us
  transfers between devices with their start and end apart: 5, of which 4 were waited for; matrix products, arithmetic and copies ran while one was open for 6% of the time, Pallas kernels for 0%

commit v1 on v0

v1 whole, which is shorter than its diff:
```python
import math

import jax
import jax.numpy as jnp
from jax import lax
from jax.sharding import Mesh, PartitionSpec as P

BF = jnp.bfloat16
F32 = jnp.float32
ORB = ("y", "xh", "core")
PLANE = ("y", "xh", "core", "pts")


def sent_to_all(x, axis):
    copies = jnp.broadcast_to(x, (lax.axis_size(axis), *x.shape))
    return lax.all_to_all(copies, axis, split_axis=0, concat_axis=0, tiled=True)


def per_device(orbitals, points, fitting, screened):
    n_grid = lax.axis_size("grid")
    n_plane = lax.axis_size(PLANE)
    grid_index = lax.axis_index("grid")
    plane_index = lax.axis_index(PLANE)
    rows_dev, width_dev = orbitals.shape
    nrows = rows_dev * n_grid
    nfull = width_dev * lax.axis_size(ORB)
    npoints = points.shape[0]
    row_block = npoints // n_plane
    column_block = npoints // n_grid
    share = nfull // (n_plane * n_grid)

    columns = sent_to_all(orbitals, "grid").reshape(nrows, width_dev)
    whole = lax.all_gather(columns, ORB, axis=1, tiled=True)
    fitted = sent_to_all(fitting, "grid").reshape(nrows, row_block)

    own = lax.dynamic_slice_in_dim(points, plane_index * row_block, row_block, 0)
    block = lax.dynamic_slice_in_dim(points, grid_index * column_block, column_block, 0)
    wanted = jnp.concatenate([own, block])
    rows = lax.broadcasted_iota(jnp.int32, (1, nrows), 1)
    choose = (wanted[:, None] == rows).astype(BF)
    picked = jnp.dot(choose, whole, preferred_element_type=F32).astype(BF)
    own_full, block_full = picked[:row_block], picked[row_block:]

    density = lax.dot_general(
        own_full, block_full, (((1,), (1,)), ((), ())), preferred_element_type=F32
    )
    masked = (density * screened.astype(F32)).astype(BF)
    partial = lax.dot_general(
        block_full, masked, (((0,), (1,)), ((), ())), preferred_element_type=F32
    ).astype(BF)
    partial = partial.reshape(n_plane, n_grid, share, row_block).transpose(1, 0, 2, 3)
    parts = lax.all_to_all(partial, "grid", 0, 0, tiled=True)
    applied = jnp.sum(parts.astype(F32), axis=0).astype(BF)
    applied = applied.reshape(n_plane * share, row_block)

    terms = lax.dot_general(
        applied, fitted, (((1,), (1,)), ((), ())), preferred_element_type=F32
    ).astype(BF)
    parts = lax.all_to_all(
        terms.reshape(n_plane, share, nrows), PLANE, 0, 0, tiled=True
    )
    exchange = -jnp.sum(parts.astype(F32), axis=0)
    matrix = jnp.dot(
        exchange.astype(BF), whole, preferred_element_type=F32
    ) / math.sqrt(nrows)
    both = jnp.stack(
        [exchange.reshape(share, n_grid, -1), matrix.reshape(share, n_grid, -1)]
    ).transpose(2, 0, 1, 3)
    both = lax.all_to_all(both, "grid", 0, 0, tiled=True)
    both = both.transpose(1, 0, 2, 3).reshape(2, n_grid * share, -1)
    return both[0], both[1]


def solution(mesh):
    n_grid, n_orb, n_pts = (mesh.shape[a] for a in ("grid", "orb", "pts"))
    fine = Mesh(
        mesh.devices.reshape(n_grid, n_orb // 4, 2, 2, n_pts),
        ("grid", "y", "xh", "core", "pts"),
    )
    in_specs = (P("grid", ORB), P(), P("grid", PLANE), P(PLANE, "grid"))
    out_specs = (P(PLANE, "grid"), P(PLANE, "grid"))
    return jax.shard_map(
        per_device, mesh=fine, in_specs=in_specs, out_specs=out_specs, check_vma=False
    )
```

time: 433 us -> 247 us (0.57)
  waiting for transfers between devices: 259 us -> 107 us
  local copies, waits for them, and re-layouts: 43.1 us -> 4.22 us
  starting transfers between devices: 21.3 us -> 3.59 us
  matrix products: 10.2 us -> 26.5 us
  blocking collectives: 74.6 us -> 89.6 us
  other arithmetic: 10.1 us -> 0.32 us
    psum x1 -> x0, waiting for transfers between devices: 82.1 us -> none  [per_device(): picked = lax.psum(selected.astype(jnp.bfloat16), 'grid')]
    all_to_all x1 -> x4, blocking collectives: 18.9 us -> 89.6 us  [the longest x1 35.1 us: per_device(): parts = lax.all_to_all(partial, 'grid', 0, 0, tiled=True)]
    all_gather x2 -> x1, waiting for transfers between devices: 147 us -> 78.5 us  [per_device(): whole = lax.all_gather(columns, ORB, axis=1, tiled=True)]
    psum x1 -> x0, blocking collectives: 55.7 us -> none  [per_device(): applied = lax.psum(partial_applied, 'grid').astype(jnp.bfloat16)]
    gather x1 -> x0, local copies, waits for them, and re-layouts: 24 us -> none  [per_device(): taken = jnp.take(orbitals, clamped, axis=0).astype(jnp.float32)]
    dot_general x3 -> x4, matrix products: 10.2 us -> 26.5 us  [the longest x1 15.1 us: per_device(): picked = jnp.dot(choose, whole, preferred_element_type=F32).astype(BF)]
    all_to_all x1 -> x0, waiting for transfers between devices: 15.6 us -> none  [per_device(): lax.all_to_all(applied, ('orb', 'pts'), split_axis=1, concat_axis=0, tile...]
    all_to_all x1, waiting for transfers between devices: 13.4 us -> 28.9 us  [sent_to_all(): return lax.all_to_all(copies, axis, split_axis=0, concat_axis=0, tiled=True)]
  transfers between devices with their start and end apart: 5 -> 2, of which waited for: 4 -> 2; matrix products, arithmetic and copies ran while one was open for 6% -> 1% of each run, Pallas kernels for 0% -> 0%
where the time goes in v1:
time: 247 us; the launch traced here: 246 us
  waiting for transfers between devices  107 us (43%)
  blocking collectives  89.6 us (36%)
  matrix products  26.5 us (11%)
  between operations  14.1 us (6%)
  local copies, waits for them, and re-layouts  4.22 us (2%)
  starting transfers between devices  3.59 us (1%)
    all_gather x1, waiting for transfers between devices, per_device(): whole = lax.all_gather(columns, ORB, axis=1, tiled=True)  78.5 us
    all_to_all x1, blocking collectives, per_device(): parts = lax.all_to_all(partial, 'grid', 0, 0, tiled=True)  35.1 us
    all_to_all x1, waiting for transfers between devices, sent_to_all(): return lax.all_to_all(copies, axis, split_axis=0, concat_axis=0, tiled=True)  28.9 us
    all_to_all x1, blocking collectives, sent_to_all(): return lax.all_to_all(copies, axis, split_axis=0, concat_axis=0, tiled=True)  25 us
    all_to_all x1, blocking collectives, per_device(): lax.all_to_all(terms.reshape(n_plane, share, nrows), PLANE, 0, 0, tiled=T...  19.1 us
    dot_general x1, matrix products, per_device(): picked = jnp.dot(choose, whole, preferred_element_type=F32).astype(BF)  15.1 us
    all_to_all x1, blocking collectives, per_device(): both = lax.all_to_all(both, 'grid', 0, 0, tiled=True)  10.4 us
    dot_general x1, matrix products, per_device(): lax.dot_general(block_full, masked, (((0,), (1,)), ((), ())), preferred_e...  6.29 us
  transfers between devices with their start and end apart: 2, of which 2 were waited for; matrix products, arithmetic and copies ran while one was open for 1% of the time, Pallas kernels for 0%

profile of v1, /device:TPU:1, one launch (start us, length us, event | category | flops | bytes accessed | tf_op | source)
XLA Modules:
  0.0 245.8 jit_solution(5545429840203284281)
XLA Ops:
  7.2 0.0 all-gather.2.cloned.1.call-start
  7.2 0.9 broadcast_in_dim.7
  8.1 25.0 %all_to_all.25 = bf16[8,256,128]{2,1,0:T(8,128)(2,1)} all-to-all(bf16[8,256,128]{2,1,0:T(8,128)(2,1)S(1)} %broadcast_in_dim.7), channel_id=1, replica_groups=mesh['grid'=8,'y'=4,'xh'=2,'core'=2,'pts'=2] {'grid'}, dimensions={0} | all-to-all | bytes 1048576 | tf_op jit(solution)/shard_map/all_to_all | solution.py:16
  33.1 0.0 all-gather.2.cloned.1.call-update
  33.2 0.8 dynamic_slice.6
  33.9 0.7 dynamic_slice.7
  34.6 0.0 copy-start.1
  34.6 78.5 %all-gather.2.cloned.1.call-done = bf16[2048,2048]{1,0:T(8,128)(2,1)} async-done(((bf16[2048,128]{1,0:T(8,128)(2,1)}), bf16[2048,2048]{1,0:T(8,128)(2,1)}) %all-gather.2.cloned.1.call-update) | async-done | bytes 8388624 | tf_op jit(solution)/shard_map/all_gather | solution.py:33
  113.2 15.1 %fusion.1 = bf16[1280,2048]{1,0:T(8,128)(2,1)} fusion(bf16[2048,2048]{1,0:T(8,128)(2,1)} %all-gather.2.cloned.1.call-done, s32[1280]{0:T(1024)S(1)} %pad_add_fusion), kind=kOutput, calls=%fused_computation.2 | convolution fusion | flops 10742661120 | bytes 13636608 | tf_op jit(solution)/shard_map/dot_general | solution.py:41
  128.3 0.0 copy-done.1
  128.3 0.0 copy-start
  128.3 6.3 %fusion.7 = bf16[2048,256]{1,0:T(8,128)(2,1)S(1)} fusion(bf16[1280,2048]{1,0:T(8,128)(2,1)} %fusion.1, bf16[256,1024]{1,0:T(8,128)(2,1)S(1)} %copy-done.1), kind=kOutput, calls=%fused_computation.8 | convolution fusion | flops 2148794368 | bytes 11010048 | tf_op jit(solution)/shard_map/dot_general | solution.py:48
  134.6 0.1 copy.9
  134.7 35.1 %all_to_all.26 = bf16[8,32,8,256]{3,2,1,0:T(8,128)(2,1)S(1)} all-to-all(bf16[8,32,8,256]{3,2,1,0:T(8,128)(2,1)S(1)} %bitcast.26), channel_id=1, replica_groups=mesh['grid'=8,'y'=4,'xh'=2,'core'=2,'pts'=2] {'grid'}, dimensions={0} | all-to-all | bytes 2097152 | tf_op jit(solution)/shard_map/all_to_all | solution.py:52
  169.8 0.0 copy-done
  169.8 1.1 broadcast_in_dim.8
  170.9 3.6 %all-to-all-start.2 = ((bf16[8,256,256]{2,1,0:T(8,128)(2,1)}), bf16[8,256,256]{2,1,0:T(8,128)(2,1)S(1)}, u32[]{:S(2)}, u32[]{:S(2)}) async-start(bf16[8,256,256]{2,1,0:T(8,128)(2,1)} %broadcast_in_dim.8), calls=%async_computation.2 | async-start | bytes 2097152 | tf_op jit(solution)/shard_map/all_to_all | solution.py:16
  174.5 0.1 reduce_sum.21
  174.7 28.9 %all-to-all-done.2 = bf16[8,256,256]{2,1,0:T(8,128)(2,1)S(1)} async-done(((bf16[8,256,256]{2,1,0:T(8,128)(2,1)}), bf16[8,256,256]{2,1,0:T(8,128)(2,1)S(1)}, u32[]{:S(2)}, u32[]{:S(2)}) %all-to-all-start.2) | async-done | bytes 1048608 | tf_op jit(solution)/shard_map/all_to_all | solution.py:16
  203.6 0.5 fusion.10
  204.1 19.1 %all_to_all.27 = bf16[32,8,2048]{2,1,0:T(8,128)(2,1)S(1)} all-to-all(bf16[32,8,2048]{2,1,0:T(8,128)(2,1)S(1)} %fusion.10), channel_id=1, replica_groups=mesh['grid'=8,'y'=4,'xh'=2,'core'=2,'pts'=2] {'y','xh','core','pts'}, dimensions={0} | all-to-all | bytes 2097152 | tf_op jit(solution)/shard_map/all_to_all | solution.py:59
  223.1 0.2 convert_reduce_fusion
  223.3 4.6 %convolution_multiply_fusion = f32[8,2048]{1,0:T(8,128)S(1)} fusion(bf16[2048,2048]{1,0:T(8,128)(2,1)} %all-gather.2.cloned.1.call-done, f32[8,2048]{1,0:T(8,128)S(1)} %convert_reduce_fusion), kind=kOutput, calls=%fused_computation.11 | convolution fusion | flops 67158016 | bytes 8519680 | tf_op jit(solution)/shard_map/dot_general | solution.py:63
  227.9 10.4 %all_to_all.28 = f32[8,2,8,256]{3,2,1,0:T(8,128)S(1)} all-to-all(f32[8,2,8,256]{3,2,1,0:T(8,128)S(1)} %maximum_bitcast_fusion), channel_id=1, replica_groups=mesh['grid'=8,'y'=4,'xh'=2,'core'=2,'pts'=2] {'grid'}, dimensions={0} | all-to-all | bytes 262144 | tf_op jit(solution)/shard_map/all_to_all | solution.py:69
  238.3 0.7 slice_bitcast_fusion
  (3 shorter events, 0.0 us)
Async XLA Ops:
  7.2 106.0 %all-gather.2.cloned.1.call-start = ((), (), s32[]{:S(2)}) async-start(), calls=%async_computation.5 | async-start | bytes 8912896 | tf_op jit(solution)/shard_map/all_gather | solution.py:33
  34.6 93.7 %copy-start.1 = (bf16[256,1024]{1,0:T(8,128)(2,1)S(1)}, bf16[256,1024]{1,0:T(8,128)(2,1)}, u32[]{:S(2)}) copy-start(bf16[256,1024]{1,0:T(8,128)(2,1)} %param.7) | copy-start | bytes 1572868
  128.3 41.5 %copy-start = (bf16[256,256]{1,0:T(8,128)(2,1)S(1)}, bf16[256,256]{1,0:T(8,128)(2,1)}, u32[]{:S(2)}) copy-start(bf16[256,256]{1,0:T(8,128)(2,1)} %param.6) | copy-start | bytes 393220
  170.9 32.7 %all-to-all-start.2 = ((bf16[8,256,256]{2,1,0:T(8,128)(2,1)}), bf16[8,256,256]{2,1,0:T(8,128)(2,1)S(1)}, u32[]{:S(2)}, u32[]{:S(2)}) async-start(bf16[8,256,256]{2,1,0:T(8,128)(2,1)} %broadcast_in_dim.8), calls=%async_computation.2 | async-start | bytes 2097152 | tf_op jit(solution)/shard_map/all_to_all | solution.py:16
Sparse Core Ops, SparseCore 0:
  33.3 79.8 all-gather.1
